TPU v7x, 32 devices: a whole 2x2x4 slice. The times are simulated.
32 devices in a mesh: grp: 2 (over y), row: 4 (over z), head: 2 (over x), br: 2 (over core).
Axes of the slice: x: 2, y: 2, z: 4, core: 2. Of those that a mesh axis runs over, the one named last changes fastest.
Arguments:
- pair_acts: float32 [16, 8, 128], P(('grp', 'row', 'head')), parts along dimension 0, may hold values from -6 to 6
- alignment: float32 [64, 8, 256], P(('grp', 'br'), ('row', 'head')), parts along dimension 0, may hold values from -6 to 6
- align_mask: int32 [64, 8], P('grp', ('row', 'head')), parts along dimension 0, may hold values from 0 to 1
- residue_mask: int32 [16], P('grp'), parts along dimension 0, may hold values from 0 to 1, as said below
- align_gain: float32 [256], replicated, may hold values from 0.25 to 1.75
- outer_in: float32 [256, 64], replicated, may hold values from -0.375 to 0.375
- outer_out: float32 [1024, 128], replicated, may hold values from -1 to 1
- tri_gain: float32 [2, 128], replicated, may hold values from 0.25 to 1.75
- tri_in: float32 [2, 128, 4, 128], P(None, None, 'br'), may hold values from -5 to 5
- tri_bias: float32 [2, 128, 4], P(None, None, 'br'), may hold values from -0.5 to 0.5
- tri_out: float32 [2, 4, 32, 128], P(None, 'br'), may hold values from -0.5 to 0.5
- pair_cotangent: float32 [16, 8, 128], P(('grp', 'row', 'head')), parts along dimension 0, may hold values from -6 to 6
Outputs:
- pair_out: float32 [16, 8, 128], P(('grp', 'row', 'head')), parts along dimension 0
- pair_grad: float32 [16, 8, 128], P(('grp', 'row', 'head')), parts along dimension 0
There are 2 independent parts, one for each index of `grp`. A program takes and returns all parts, laid end to end along the dimension named above; an argument that names none is the same for every part. Nothing has to cross between parts.
Inputs may be any that keep to these rules, and one draw needn't show every extreme that they name: `residue_mask`: 1 at residue 0, and 0 at one or more residues; `align_mask`: 1 at every residue of sequence 0 of each part.
All inputs are finite; a program needn't handle non-finite values.
Results may differ from a plain program's by a relative error of at most 0.0003.
Values sent between devices are 32-bit elements; how exact they have to be, the bound alone decides.
No kernel may reach another device: no remote copies, remote signals or barrier semaphores. Data moves between devices by JAX's collectives and lax.ppermute only.
A program may use at most 64 MiB of HBM per device.

v0:
```python
import jax
import jax.numpy as jnp
from jax import lax
from jax.sharding import PartitionSpec as P

OPC = 32
PRECISE = lax.Precision.HIGHEST
EPSILON = 1e-05
MASK_SHIFT = 1000000000.0


def normalize(values, scales):
    average = jnp.mean(values, axis=-1, keepdims=True)
    centred = values - average
    spread = jnp.mean(centred * centred, axis=-1, keepdims=True)
    return centred * lax.rsqrt(spread + EPSILON) * scales


def core_total(values):
    return lax.psum(values, "br")


def reorient(values):
    turned = jnp.swapaxes(values, 0, 1)
    return lax.all_to_all(turned, ("row", "head"), split_axis=0, concat_axis=1, tiled=True)


def prepare(values, scales, weight_in, weight_bias):
    normed = normalize(values, scales)
    projected = jnp.einsum("ijc,chd->ijhd", normed, weight_in, precision=PRECISE)
    bias_local = jnp.einsum("jkc,ch->hjk", normed, weight_bias, precision=PRECISE)
    return (projected, bias_local)


def attend(projected, bias_full, key_shift, weight_out):
    head_size = projected.shape[-1] // 4
    queries = projected[..., :head_size]
    key_proj = projected[..., head_size : 2 * head_size]
    value_proj = projected[..., 2 * head_size : 3 * head_size]
    gating = projected[..., 3 * head_size :]
    logits = jnp.einsum("ijhd,ikhd->ihjk", queries, key_proj, precision=PRECISE) * head_size ** (
        -0.5
    )
    logits = logits + bias_full[None] + key_shift
    attention = jax.nn.softmax(logits, axis=-1)
    attended = jnp.einsum("ihjk,ikhd->ijhd", attention, value_proj, precision=PRECISE)
    gated_out = jax.nn.sigmoid(gating) * attended
    return jnp.einsum("ijhd,hdc->ijc", gated_out, weight_out, precision=PRECISE)


def tri_forward(rows_in, scales, weight_in, weight_bias, weight_out, key_shift, pair_mask):

    def local_prep(values):
        return prepare(values, scales, weight_in, weight_bias)

    (projected, bias_local), pull_prep = jax.vjp(local_prep, rows_in)
    bias_full = lax.all_gather(bias_local, ("row", "head"), axis=1, tiled=True)

    def local_attend(proj_in, bias_in):
        return attend(proj_in, bias_in, key_shift, weight_out)

    partial_out, pull_attend = jax.vjp(local_attend, projected, bias_full)
    total_out = core_total(partial_out)
    return (rows_in + total_out * pair_mask, (pull_prep, pull_attend))


def tri_backward(grad_out, saved, pair_mask):
    pull_prep, pull_attend = saved
    grad_proj, grad_bias = pull_attend(grad_out * pair_mask)
    grad_local = lax.psum_scatter(grad_bias, ("row", "head"), scatter_dimension=1, tiled=True)
    (grad_rows,) = pull_prep((grad_proj, grad_local))
    return grad_out + core_total(grad_rows)


def body(
    pair_acts,
    alignment,
    align_mask,
    residue_mask,
    align_gain,
    outer_in,
    outer_out,
    tri_gain,
    tri_in,
    tri_bias,
    tri_out,
    pair_cotangent,
):
    row_count = pair_acts.shape[0]
    live = residue_mask.astype(jnp.float32)
    key_shift = (live - 1.0) * MASK_SHIFT
    row_live = lax.dynamic_slice_in_dim(
        live, lax.axis_index(("row", "head")) * row_count, row_count, 0
    )
    pair_mask = row_live[:, None, None] * live[None, :, None]
    seq_count = alignment.shape[0]
    mask_all = align_mask.astype(jnp.float32)
    mask_own = lax.dynamic_slice_in_dim(mask_all, lax.axis_index("br") * seq_count, seq_count, 0)
    normed = normalize(alignment, align_gain)
    projected = jnp.einsum("snc,ck->snk", normed, outer_in, precision=PRECISE)
    left_part = projected[..., :OPC] * mask_own[..., None]
    right_part = jnp.swapaxes(projected[..., OPC:] * mask_own[..., None], 1, 2)
    right_all, mask_cols = (
        lax.all_gather(right_part, ("row", "head"), axis=2, tiled=True),
        lax.all_gather(mask_all, ("row", "head"), axis=1, tiled=True),
    )
    counts = jnp.einsum("si,sj->ij", mask_all, mask_cols, precision=PRECISE)
    table = outer_out.reshape(OPC, OPC, outer_out.shape[-1])
    mixed_left = jnp.einsum("sip,pqc->siqc", left_part, table, precision=PRECISE)
    partial_outer = jnp.einsum("siqc,sqj->ijc", mixed_left, right_all, precision=PRECISE)
    outer_sum = core_total(partial_outer)
    pair_one = pair_acts + outer_sum / counts[..., None]
    pair_two, saved_start = tri_forward(
        pair_one, tri_gain[0], tri_in[0], tri_bias[0], tri_out[0], key_shift, pair_mask
    )
    turned_two = reorient(pair_two)
    turned_three, saved_end = tri_forward(
        turned_two, tri_gain[1], tri_in[1], tri_bias[1], tri_out[1], key_shift, pair_mask
    )
    pair_out = reorient(turned_three)
    grad_turned = reorient(pair_cotangent)
    grad_turned = tri_backward(grad_turned, saved_end, pair_mask)
    grad_two = reorient(grad_turned)
    pair_grad = tri_backward(grad_two, saved_start, pair_mask)
    return (pair_out, pair_grad)


def solution(mesh):
    in_specs = (
        P(("grp", "row", "head"), None, None),
        P(("grp", "br"), ("row", "head"), None),
        P("grp", ("row", "head")),
        P("grp"),
        P(),
        P(),
        P(),
        P(),
        P(None, None, "br", None),
        P(None, None, "br"),
        P(None, "br", None, None),
        P(("grp", "row", "head"), None, None),
    )
    out_specs = (P(("grp", "row", "head"), None, None), P(("grp", "row", "head"), None, None))
    return jax.shard_map(body, mesh=mesh, in_specs=in_specs, out_specs=out_specs, check_vma=False)
```

profile of v0, /device:TPU:0, one launch (start us, length us, event | category | flops | bytes accessed | tf_op | source)
XLA Modules:
  0.0 188.4 jit_solution(10134027815885279675)
XLA Ops:
  0.7 1.0 reduce_sum.121
  1.7 0.3 multiply_reduce_fusion
  2.0 0.7 convert_bitcast_fusion
  2.6 0.8 multiply_multiply_fusion
  3.7 32.3 %all_gather.12 = f32[16,32,8]{1,0,2:T(8,128)S(1)} all-gather(f32[16,32,1]{1,0,2:T(8,128)S(1)} %fusion.30), channel_id=1, replica_groups=mesh['grp'=2,'row'=4,'head'=2,'br'=2] {'row','head'}, dimensions={2}, use_global_device_ids=true | all-gather | bytes 18432 | tf_op jit(solution)/shard_map/all_gather | solution.py:104
  36.2 0.7 fusion.8
  36.9 0.7 convolution_bitcast_fusion.17
  37.6 2.5 %psum.35 = f32[1,8,128]{2,1,0:T(8,128)S(1)} all-reduce(f32[1,8,128]{2,1,0:T(8,128)S(1)} %convolution_bitcast_fusion.17), channel_id=1, replica_groups=mesh['grp'=2,'row'=4,'head'=2,'br'=2] {'br'}, use_global_device_ids=true, to_apply=%region_2.0 | all-reduce | flops 1024 | bytes 8192 | tf_op jit(solution)/shard_map/psum | solution.py:20
  40.0 20.4 %all-gather.2 = f32[8,1,32]{2,1,0:T(1,128)S(1)} all-gather(f32[1,1,32]{2,1,0:T(1,128)S(1)} %get-tuple-element.16), channel_id=1, replica_groups=mesh['grp'=2,'row'=4,'head'=2,'br'=2] {'row','head'}, dimensions={0}, use_global_device_ids=true | all-gather | bytes 1152 | tf_op jit(solution)/shard_map/all_gather | solution.py:105
  60.5 0.7 copy-done.8
  61.3 0.6 copy-done.7
  62.4 0.6 copy-done.9
  63.0 0.6 dynamic_slice.7
  63.6 0.6 broadcast_multiply_fusion.2
  64.5 0.5 copy-done.5
  65.1 16.3 %all-gather.3 = f32[8,8,2]{1,2,0:T(2,128)S(1)} all-gather(f32[1,8,2]{1,2,0:T(2,128)S(1)} %convolution_bitcast_fusion.19), channel_id=2, replica_groups=mesh['grp'=2,'row'=4,'head'=2,'br'=2] {'row','head'}, dimensions={0}, use_global_device_ids=true | all-gather | bytes 576 | tf_op jit(solution)/shard_map/all_gather | solution.py:57
  82.1 0.4 copy-done.2
  82.5 0.3 convolution_bitcast_fusion.16
  82.8 2.5 %psum.36 = f32[1,8,128]{2,1,0:T(8,128)S(1)} all-reduce(f32[1,8,128]{2,1,0:T(8,128)S(1)} %convolution_bitcast_fusion.16), channel_id=1, replica_groups=mesh['grp'=2,'row'=4,'head'=2,'br'=2] {'br'}, use_global_device_ids=true, to_apply=%region_7.0 | all-reduce | flops 1024 | bytes 8192 | tf_op jit(solution)/shard_map/psum | solution.py:20
  85.2 0.7 multiply_add_fusion
  85.9 3.3 %all-to-all-start = ((f32[8,1,128]{2,1,0:T(1,128)}), f32[8,1,128]{2,1,0:T(1,128)S(1)}, u32[]{:S(2)}, u32[]{:S(2)}) async-start(f32[8,1,128]{2,1,0:T(1,128)} %bitcast.32), calls=%async_computation | async-start | bytes 8192 | tf_op jit(solution)/shard_map/all_to_all | solution.py:25
  89.3 0.6 copy-done.10
  89.9 0.6 dynamic-slice
  90.5 5.1 %all-to-all-done = f32[8,1,128]{2,1,0:T(1,128)S(1)} async-done(((f32[8,1,128]{2,1,0:T(1,128)}), f32[8,1,128]{2,1,0:T(1,128)S(1)}, u32[]{:S(2)}, u32[]{:S(2)}) %all-to-all-start) | async-done | bytes 4128 | tf_op jit(solution)/shard_map/all_to_all | solution.py:25
  95.6 3.3 %all-to-all-start.2 = ((f32[8,1,128]{2,1,0:T(1,128)}), f32[8,1,128]{2,1,0:T(1,128)S(1)}, u32[]{:S(2)}, u32[]{:S(2)}) async-start(f32[8,1,128]{2,1,0:T(1,128)} %bitcast.54), calls=%async_computation.2 | async-start | bytes 8192 | tf_op jit(solution)/shard_map/all_to_all | solution.py:25
  99.5 20.9 %all-gather.4 = f32[8,8,2]{1,2,0:T(2,128)S(1)} all-gather(f32[1,8,2]{1,2,0:T(2,128)S(1)} %convolution_bitcast_fusion.18), channel_id=3, replica_groups=mesh['grp'=2,'row'=4,'head'=2,'br'=2] {'row','head'}, dimensions={0}, use_global_device_ids=true | all-gather | bytes 576 | tf_op jit(solution)/shard_map/all_gather | solution.py:57
  120.8 0.2 fusion.123
  121.7 0.3 multiply_reduce_fusion.2
  122.4 0.2 convolution_bitcast_fusion.6
  122.7 17.4 %all-reduce.8 = f32[2,8,8]{2,0,1:T(2,128)S(1)} all-reduce(f32[2,8,8]{2,0,1:T(2,128)S(1)} %copy.49), channel_id=4, replica_groups=mesh['grp'=2,'row'=4,'head'=2,'br'=2] {'row','head'}, use_global_device_ids=true, to_apply=%region_14.0.clone | all-reduce | flops 128 | bytes 1024
  140.0 0.8 fusion.92
  140.9 0.4 multiply_reduce_fusion.3
  141.6 2.5 %psum.38 = f32[1,8,128]{2,1,0:T(8,128)S(1)} all-reduce(f32[1,8,128]{2,1,0:T(8,128)S(1)} %add_bitcast_fusion), channel_id=1, replica_groups=mesh['grp'=2,'row'=4,'head'=2,'br'=2] {'br'}, use_global_device_ids=true, to_apply=%region_17.0 | all-reduce | flops 1024 | bytes 8192 | tf_op jit(solution)/shard_map/psum | solution.py:20
  144.0 0.6 bitcast_add_fusion.1
  144.6 3.3 %all-to-all-start.3 = ((f32[8,1,128]{2,1,0:T(1,128)}), f32[8,1,128]{2,1,0:T(1,128)S(1)}, u32[]{:S(2)}, u32[]{:S(2)}) async-start(f32[8,1,128]{2,1,0:T(1,128)} %bitcast.75), calls=%async_computation.3 | async-start | bytes 8192 | tf_op jit(solution)/shard_map/all_to_all | solution.py:25
  147.9 0.3 convolution_bitcast_fusion.15
  148.2 6.1 %all-to-all-done.3 = f32[8,1,128]{2,1,0:T(1,128)S(1)} async-done(((f32[8,1,128]{2,1,0:T(1,128)}), f32[8,1,128]{2,1,0:T(1,128)S(1)}, u32[]{:S(2)}, u32[]{:S(2)}) %all-to-all-start.3) | async-done | bytes 4128 | tf_op jit(solution)/shard_map/all_to_all | solution.py:25
  154.6 0.3 multiply_reduce_fusion.1
  155.3 0.2 convolution_bitcast_fusion.2
  155.6 17.9 %all-reduce.9 = f32[2,8,8]{2,0,1:T(2,128)S(1)} all-reduce(f32[2,8,8]{2,0,1:T(2,128)S(1)} %copy.52), channel_id=5, replica_groups=mesh['grp'=2,'row'=4,'head'=2,'br'=2] {'row','head'}, use_global_device_ids=true, to_apply=%region_19.0.clone | all-reduce | flops 128 | bytes 1024
  173.5 0.8 fusion.91
  174.4 0.4 fusion.65
  175.1 2.5 %all-reduce.10 = (f32[1,8,128]{2,1,0:T(8,128)S(1)}, f32[1,8,128]{2,1,0:T(8,128)S(1)}) all-reduce(f32[1,8,128]{2,1,0:T(8,128)S(1)} %convolution_bitcast_fusion.15, f32[1,8,128]{2,1,0:T(8,128)S(1)} %broadcast_add_fusion), channel_id=1, replica_groups=mesh['grp'=2,'row'=4,'head'=2,'br'=2] {'br'}, use_global_device_ids=true, to_apply=%region_12.0 | all-reduce | flops 2048 | bytes 16384 | tf_op jit(solution)/shard_map/psum | solution.py:20
  177.5 0.7 bitcast_add_fusion.2
  178.2 3.3 %all-to-all-start.1 = ((f32[8,1,128]{2,1,0:T(1,128)}), f32[8,1,128]{2,1,0:T(1,128)S(1)}, u32[]{:S(2)}, u32[]{:S(2)}) async-start(f32[8,1,128]{2,1,0:T(1,128)} %bitcast.52), calls=%async_computation.1 | async-start | bytes 8192 | tf_op jit(solution)/shard_map/all_to_all | solution.py:25
  181.5 0.6 bitcast_add_fusion
  182.1 5.8 %all-to-all-done.1 = f32[8,1,128]{2,1,0:T(1,128)S(1)} async-done(((f32[8,1,128]{2,1,0:T(1,128)}), f32[8,1,128]{2,1,0:T(1,128)S(1)}, u32[]{:S(2)}, u32[]{:S(2)}) %all-to-all-start.1) | async-done | bytes 4128 | tf_op jit(solution)/shard_map/all_to_all | solution.py:25
  187.9 0.6 copy.81
  (77 shorter events, 5.4 us)
Async XLA Ops:
  0.6 35.6 %copy-start = (f32[1024,128]{1,0:T(8,128)S(1)}, f32[1024,128]{1,0:T(8,128)}, u32[]{:S(2)}) copy-start(f32[1024,128]{1,0:T(8,128)} %param.18) | copy-start | bytes 1572868
  0.6 1.0 copy-start.3
  0.7 2.8 %copy-start.4 = (f32[256,64]{0,1:T(8,128)S(1)}, f32[256,64]{0,1:T(8,128)}, u32[]{:S(2)}) copy-start(f32[256,64]{0,1:T(8,128)} %param.17) | copy-start | bytes 196612
  36.9 24.4 %copy-start.1 = (f32[2,128,2,128]{3,2,1,0:T(2,128)S(1)}, f32[2,128,2,128]{3,2,1,0:T(2,128)}, u32[]{:S(2)}) copy-start(f32[2,128,2,128]{3,2,1,0:T(2,128)} %param.20) | copy-start | bytes 786436
  60.5 0.7 copy-start.8
  61.2 0.7 copy-start.7
  61.2 0.7 copy-start.6
  62.3 0.7 copy-start.9
  64.2 0.7 copy-start.5
  81.7 0.8 copy-start.2
  85.9 9.7 %all-to-all-start = ((f32[8,1,128]{2,1,0:T(1,128)}), f32[8,1,128]{2,1,0:T(1,128)S(1)}, u32[]{:S(2)}, u32[]{:S(2)}) async-start(f32[8,1,128]{2,1,0:T(1,128)} %bitcast.32), calls=%async_computation | async-start | bytes 8192 | tf_op jit(solution)/shard_map/all_to_all | solution.py:25
  89.2 0.7 copy-start.10
  95.6 25.7 %all-to-all-start.2 = ((f32[8,1,128]{2,1,0:T(1,128)}), f32[8,1,128]{2,1,0:T(1,128)S(1)}, u32[]{:S(2)}, u32[]{:S(2)}) async-start(f32[8,1,128]{2,1,0:T(1,128)} %bitcast.54), calls=%async_computation.2 | async-start | bytes 8192 | tf_op jit(solution)/shard_map/all_to_all | solution.py:25
  144.6 9.7 %all-to-all-start.3 = ((f32[8,1,128]{2,1,0:T(1,128)}), f32[8,1,128]{2,1,0:T(1,128)S(1)}, u32[]{:S(2)}, u32[]{:S(2)}) async-start(f32[8,1,128]{2,1,0:T(1,128)} %bitcast.75), calls=%async_computation.3 | async-start | bytes 8192 | tf_op jit(solution)/shard_map/all_to_all | solution.py:25
  178.2 9.7 %all-to-all-start.1 = ((f32[8,1,128]{2,1,0:T(1,128)}), f32[8,1,128]{2,1,0:T(1,128)S(1)}, u32[]{:S(2)}, u32[]{:S(2)}) async-start(f32[8,1,128]{2,1,0:T(1,128)} %bitcast.52), calls=%async_computation.1 | async-start | bytes 8192 | tf_op jit(solution)/shard_map/all_to_all | solution.py:25
where the time goes:
time: 189 us; the launch traced here: 188 us
  blocking collectives  135 us (71%)
  waiting for transfers between devices  17 us (9%)
  starting transfers between devices  13.2 us (7%)
  matrix products  8.39 us (4%)
  other arithmetic  7.59 us (4%)
  local copies, waits for them, and re-layouts  6.07 us (3%)
    all_gather x2, blocking collectives, tri_forward(): bias_full = lax.all_gather(bias_local, ('row', 'head'), axis=1, tiled=True)  37.2 us
    unnamed x2, blocking collectives  35.3 us
    all_gather x1, blocking collectives, body(): lax.all_gather(right_part, ('row', 'head'), axis=2, tiled=True)  32.3 us
    all_gather x1, blocking collectives, body(): lax.all_gather(mask_all, ('row', 'head'), axis=1, tiled=True)  20.4 us
    all_to_all x4, waiting for transfers between devices, reorient(): lax.all_to_all(turned, ('row', 'head'), split_axis=0, concat_axis=1, tile...  17 us
    all_to_all x4, starting transfers between devices, reorient(): lax.all_to_all(turned, ('row', 'head'), split_axis=0, concat_axis=1, tile...  13.2 us
    psum x4, blocking collectives, core_total(): return lax.psum(values, 'br')  9.82 us
    unnamed x26, local copies, waits for them, and re-layouts  4.8 us
  transfers between devices with their start and end apart: 4, of which 3 were waited for; matrix products, arithmetic and copies ran while one was open for 2% of the time, Pallas kernels for 0%

commit v1 on v0

--- a/solution.py
+++ b/solution.py
@@ -22,7 +22,16 @@
 
 def reorient(values):
     turned = jnp.swapaxes(values, 0, 1)
-    return lax.all_to_all(turned, ("row", "head"), split_axis=0, concat_axis=1, tiled=True)
+    try_all_tokens = lambda along_dim, row_dim, array_in: jnp.concatenate(
+        lax.all_to_all(
+            jnp.stack(jnp.split(array_in, lax.axis_size(("row", "head")), along_dim), axis=0),
+            axis_name=("row", "head"),
+            split_axis=0,
+            concat_axis=0,
+        ),
+        row_dim,
+    )
+    return try_all_tokens(0, 1, turned)
 
 
 def prepare(values, scales, weight_in, weight_bias):

time: 189 us -> 202 us (1.069)
  local copies, waits for them, and re-layouts: 6.07 us -> 22.6 us
  waiting for transfers between devices: 17 us -> 12.8 us
    unnamed x26 -> x56, local copies, waits for them, and re-layouts: 4.8 us -> 19.3 us
    all_to_all x4, waiting for transfers between devices: 17 us -> 12.8 us  [reorient(): lax.all_to_all(jnp.stack(jnp.split(array_in, lax.axis_size(('row', 'head'...]
    another operation x0 -> x4, local copies, waits for them, and re-layouts: none -> 2.05 us  [reorient(): jnp.stack(jnp.split(array_in, lax.axis_size(('row', 'head')), along_dim),...]
  transfers between devices with their start and end apart: 4 -> 4, of which waited for: 3 -> 3; matrix products, arithmetic and copies ran while one was open for 2% -> 4% of each run, Pallas kernels for 0% -> 0%
where the time goes in v1:
time: 202 us; the launch traced here: 201 us
  blocking collectives  135 us (67%)
  local copies, waits for them, and re-layouts  22.6 us (11%)
  starting transfers between devices  15.1 us (7%)
  waiting for transfers between devices  12.8 us (6%)
  matrix products  8.47 us (4%)
  other arithmetic  5.81 us (3%)
    all_gather x2, blocking collectives, tri_forward(): bias_full = lax.all_gather(bias_local, ('row', 'head'), axis=1, tiled=True)  37.3 us
    unnamed x2, blocking collectives  35.4 us
    all_gather x1, blocking collectives, body(): lax.all_gather(right_part, ('row', 'head'), axis=2, tiled=True)  32.3 us
    all_gather x1, blocking collectives, body(): lax.all_gather(mask_all, ('row', 'head'), axis=1, tiled=True)  20.4 us
    unnamed x56, local copies, waits for them, and re-layouts  19.3 us
    all_to_all x4, starting transfers between devices, reorient(): lax.all_to_all(jnp.stack(jnp.split(array_in, lax.axis_size(('row', 'head'...  15.1 us
    all_to_all x4, waiting for transfers between devices, reorient(): lax.all_to_all(jnp.stack(jnp.split(array_in, lax.axis_size(('row', 'head'...  12.8 us
    psum x4, blocking collectives, core_total(): return lax.psum(values, 'br')  9.82 us
  transfers between devices with their start and end apart: 4, of which 3 were waited for; matrix products, arithmetic and copies ran while one was open for 4% of the time, Pallas kernels for 0%

profile of v1, /device:TPU:0, one launch (start us, length us, event | category | flops | bytes accessed | tf_op | source)
XLA Modules:
  0.0 201.0 jit_solution(3927928212251576341)
XLA Ops:
  0.7 1.0 reduce_sum.121
  2.0 0.7 convert_bitcast_fusion
  2.6 0.8 multiply_multiply_fusion
  3.7 32.3 %all_gather.12 = f32[16,32,8]{1,0,2:T(8,128)S(1)} all-gather(f32[16,32,1]{1,0,2:T(8,128)S(1)} %fusion.30), channel_id=1, replica_groups=mesh['grp'=2,'row'=4,'head'=2,'br'=2] {'row','head'}, dimensions={2}, use_global_device_ids=true | all-gather | bytes 18432 | tf_op jit(solution)/shard_map/all_gather | solution.py:113
  36.2 0.7 fusion.8
  36.9 0.7 convolution_bitcast_fusion.17
  37.6 2.5 %psum.35 = f32[1,8,128]{2,1,0:T(8,128)S(1)} all-reduce(f32[1,8,128]{2,1,0:T(8,128)S(1)} %convolution_bitcast_fusion.17), channel_id=1, replica_groups=mesh['grp'=2,'row'=4,'head'=2,'br'=2] {'br'}, use_global_device_ids=true, to_apply=%region_2.0 | all-reduce | flops 1024 | bytes 8192 | tf_op jit(solution)/shard_map/psum | solution.py:20
  40.0 20.4 %all-gather.2 = f32[8,1,32]{2,1,0:T(1,128)S(1)} all-gather(f32[1,1,32]{2,1,0:T(1,128)S(1)} %get-tuple-element.16), channel_id=1, replica_groups=mesh['grp'=2,'row'=4,'head'=2,'br'=2] {'row','head'}, dimensions={0}, use_global_device_ids=true | all-gather | bytes 1152 | tf_op jit(solution)/shard_map/all_gather | solution.py:114
  60.5 0.7 copy-done.8
  61.3 0.6 copy-done.7
  62.4 0.6 copy-done.9
  63.0 0.6 dynamic_slice.7
  63.6 0.6 broadcast_multiply_fusion.2
  65.1 16.3 %all-gather.3 = f32[8,8,2]{1,2,0:T(2,128)S(1)} all-gather(f32[1,8,2]{1,2,0:T(2,128)S(1)} %convolution_bitcast_fusion.19), channel_id=2, replica_groups=mesh['grp'=2,'row'=4,'head'=2,'br'=2] {'row','head'}, dimensions={0}, use_global_device_ids=true | all-gather | bytes 576 | tf_op jit(solution)/shard_map/all_gather | solution.py:66
  82.8 2.5 %psum.36 = f32[1,8,128]{2,1,0:T(8,128)S(1)} all-reduce(f32[1,8,128]{2,1,0:T(8,128)S(1)} %convolution_bitcast_fusion.16), channel_id=1, replica_groups=mesh['grp'=2,'row'=4,'head'=2,'br'=2] {'br'}, use_global_device_ids=true, to_apply=%region_7.0 | all-reduce | flops 1024 | bytes 8192 | tf_op jit(solution)/shard_map/psum | solution.py:20
  85.3 0.5 constant_dynamic-update-slice_fusion.7
  87.9 0.5 constant_dynamic-update-slice_fusion.2
  88.4 0.5 constant_dynamic-update-slice_fusion.1
  88.9 0.5 constant_dynamic-update-slice_fusion
  89.4 3.4 %all-to-all-start = ((f32[8,1,1,128]{3,2,1,0:T(1,128)}), f32[8,1,1,128]{3,2,1,0:T(1,128)S(1)}, u32[]{:S(2)}, u32[]{:S(2)}) async-start(f32[8,1,1,128]{3,2,1,0:T(1,128)} %constant_dynamic-update-slice_fusion), calls=%async_computation | async-start | bytes 8192 | tf_op jit(solution)/shard_map/all_to_all | solution.py:26
  92.9 0.5 constant_dynamic-update-slice_fusion.23
  93.4 0.5 constant_dynamic-update-slice_fusion.22
  93.9 0.5 constant_dynamic-update-slice_fusion.21
  94.4 0.5 constant_dynamic-update-slice_fusion.20
  94.9 0.5 constant_dynamic-update-slice_fusion.19
  97.0 0.7 copy-done.11
  97.7 0.7 dynamic-slice
  98.3 0.9 all-to-all-done
  99.3 5.0 %all-to-all-start.2 = ((f32[8,1,1,128]{3,2,1,0:T(1,128)}), f32[8,1,1,128]{3,2,1,0:T(1,128)S(1)}, u32[]{:S(2)}, u32[]{:S(2)}) async-start(f32[8,1,1,128]{3,2,1,0:T(1,128)} %constant_dynamic-update-slice_fusion.16), calls=%async_computation.2 | async-start | bytes 8192 | tf_op jit(solution)/shard_map/all_to_all | solution.py:26
  104.8 21.0 %all-gather.4 = f32[8,8,2]{1,2,0:T(2,128)S(1)} all-gather(f32[1,8,2]{1,2,0:T(2,128)S(1)} %convolution_bitcast_fusion.18), channel_id=3, replica_groups=mesh['grp'=2,'row'=4,'head'=2,'br'=2] {'row','head'}, dimensions={0}, use_global_device_ids=true | all-gather | bytes 576 | tf_op jit(solution)/shard_map/all_gather | solution.py:66
  128.1 17.4 %all-reduce.8 = f32[2,8,8]{2,0,1:T(2,128)S(1)} all-reduce(f32[2,8,8]{2,0,1:T(2,128)S(1)} %copy.95), channel_id=4, replica_groups=mesh['grp'=2,'row'=4,'head'=2,'br'=2] {'row','head'}, use_global_device_ids=true, to_apply=%region_14.0.clone | all-reduce | flops 128 | bytes 1024
  145.5 0.9 fusion.90
  147.1 2.5 %psum.38 = f32[1,8,128]{2,1,0:T(8,128)S(1)} all-reduce(f32[1,8,128]{2,1,0:T(8,128)S(1)} %add_bitcast_fusion), channel_id=1, replica_groups=mesh['grp'=2,'row'=4,'head'=2,'br'=2] {'br'}, use_global_device_ids=true, to_apply=%region_17.0 | all-reduce | flops 1024 | bytes 8192 | tf_op jit(solution)/shard_map/psum | solution.py:20
  149.5 0.5 constant_dynamic-update-slice_fusion.31
  150.0 0.5 constant_dynamic-update-slice_fusion.30
  150.6 0.5 constant_dynamic-update-slice_fusion.29
  151.1 0.5 constant_dynamic-update-slice_fusion.28
  151.6 0.5 constant_dynamic-update-slice_fusion.27
  153.6 3.3 %all-to-all-start.3 = ((f32[8,1,1,128]{3,2,1,0:T(1,128)}), f32[8,1,1,128]{3,2,1,0:T(1,128)S(1)}, u32[]{:S(2)}, u32[]{:S(2)}) async-start(f32[8,1,1,128]{3,2,1,0:T(1,128)} %constant_dynamic-update-slice_fusion.24), calls=%async_computation.3 | async-start | bytes 8192 | tf_op jit(solution)/shard_map/all_to_all | solution.py:26
  157.2 6.1 %all-to-all-done.3 = f32[8,1,1,128]{3,2,1,0:T(1,128)S(1)} async-done(((f32[8,1,1,128]{3,2,1,0:T(1,128)}), f32[8,1,1,128]{3,2,1,0:T(1,128)S(1)}, u32[]{:S(2)}, u32[]{:S(2)}) %all-to-all-start.3) | async-done | bytes 4128 | tf_op jit(solution)/shard_map/all_to_all | solution.py:26
  164.6 17.9 %all-reduce.9 = f32[2,8,8]{2,0,1:T(2,128)S(1)} all-reduce(f32[2,8,8]{2,0,1:T(2,128)S(1)} %copy.97), channel_id=5, replica_groups=mesh['grp'=2,'row'=4,'head'=2,'br'=2] {'row','head'}, use_global_device_ids=true, to_apply=%region_19.0.clone | all-reduce | flops 128 | bytes 1024
  182.5 0.9 fusion.89
  184.1 2.5 %all-reduce.10 = (f32[1,8,128]{2,1,0:T(8,128)S(1)}, f32[1,8,128]{2,1,0:T(8,128)S(1)}) all-reduce(f32[1,8,128]{2,1,0:T(8,128)S(1)} %convolution_bitcast_fusion.15, f32[1,8,128]{2,1,0:T(8,128)S(1)} %broadcast_add_fusion), channel_id=1, replica_groups=mesh['grp'=2,'row'=4,'head'=2,'br'=2] {'br'}, use_global_device_ids=true, to_apply=%region_12.0 | all-reduce | flops 2048 | bytes 16384 | tf_op jit(solution)/shard_map/psum | solution.py:20
  186.6 0.5 constant_dynamic-update-slice_fusion.15
  190.7 3.3 %all-to-all-start.1 = ((f32[8,1,1,128]{3,2,1,0:T(1,128)}), f32[8,1,1,128]{3,2,1,0:T(1,128)S(1)}, u32[]{:S(2)}, u32[]{:S(2)}) async-start(f32[8,1,1,128]{3,2,1,0:T(1,128)} %constant_dynamic-update-slice_fusion.8), calls=%async_computation.1 | async-start | bytes 8192 | tf_op jit(solution)/shard_map/all_to_all | solution.py:26
  194.0 0.6 add.132
  194.6 5.8 %all-to-all-done.1 = f32[8,1,1,128]{3,2,1,0:T(1,128)S(1)} async-done(((f32[8,1,1,128]{3,2,1,0:T(1,128)}), f32[8,1,1,128]{3,2,1,0:T(1,128)S(1)}, u32[]{:S(2)}, u32[]{:S(2)}) %all-to-all-start.1) | async-done | bytes 4128 | tf_op jit(solution)/shard_map/all_to_all | solution.py:26
  200.4 0.6 copy.154
  (111 shorter events, 18.0 us)
Async XLA Ops:
  0.6 35.6 %copy-start = (f32[1024,128]{1,0:T(8,128)S(1)}, f32[1024,128]{1,0:T(8,128)}, u32[]{:S(2)}) copy-start(f32[1024,128]{1,0:T(8,128)} %param.18) | copy-start | bytes 1572868
  0.6 1.0 copy-start.3
  0.7 2.8 %copy-start.4 = (f32[256,64]{0,1:T(8,128)S(1)}, f32[256,64]{0,1:T(8,128)}, u32[]{:S(2)}) copy-start(f32[256,64]{0,1:T(8,128)} %param.17) | copy-start | bytes 196612
  36.9 24.4 %copy-start.1 = (f32[2,128,2,128]{3,2,1,0:T(2,128)S(1)}, f32[2,128,2,128]{3,2,1,0:T(2,128)}, u32[]{:S(2)}) copy-start(f32[2,128,2,128]{3,2,1,0:T(2,128)} %param.20) | copy-start | bytes 786436
  60.5 0.7 copy-start.8
  61.2 0.7 copy-start.7
  61.2 0.7 copy-start.6
  62.3 0.7 copy-start.9
  64.2 0.7 copy-start.5
  81.7 0.8 copy-start.2
  89.4 3.5 %copy-start.10 = (f32[1,8,128]{2,1,0:T(8,128)S(1)}, f32[1,8,128]{2,1,0:T(8,128)}, u32[]{:S(2)}) copy-start(f32[1,8,128]{2,1,0:T(8,128)} %param.23) | copy-start | bytes 12292
  89.4 9.8 %all-to-all-start = ((f32[8,1,1,128]{3,2,1,0:T(1,128)}), f32[8,1,1,128]{3,2,1,0:T(1,128)S(1)}, u32[]{:S(2)}, u32[]{:S(2)}) async-start(f32[8,1,1,128]{3,2,1,0:T(1,128)} %constant_dynamic-update-slice_fusion), calls=%async_computation | async-start | bytes 8192 | tf_op jit(solution)/shard_map/all_to_all | solution.py:26
  97.0 0.7 copy-start.11
  99.3 27.5 %all-to-all-start.2 = ((f32[8,1,1,128]{3,2,1,0:T(1,128)}), f32[8,1,1,128]{3,2,1,0:T(1,128)S(1)}, u32[]{:S(2)}, u32[]{:S(2)}) async-start(f32[8,1,1,128]{3,2,1,0:T(1,128)} %constant_dynamic-update-slice_fusion.16), calls=%async_computation.2 | async-start | bytes 8192 | tf_op jit(solution)/shard_map/all_to_all | solution.py:26
  153.6 9.7 %all-to-all-start.3 = ((f32[8,1,1,128]{3,2,1,0:T(1,128)}), f32[8,1,1,128]{3,2,1,0:T(1,128)S(1)}, u32[]{:S(2)}, u32[]{:S(2)}) async-start(f32[8,1,1,128]{3,2,1,0:T(1,128)} %constant_dynamic-update-slice_fusion.24), calls=%async_computation.3 | async-start | bytes 8192 | tf_op jit(solution)/shard_map/all_to_all | solution.py:26
  190.7 9.7 %all-to-all-start.1 = ((f32[8,1,1,128]{3,2,1,0:T(1,128)}), f32[8,1,1,128]{3,2,1,0:T(1,128)S(1)}, u32[]{:S(2)}, u32[]{:S(2)}) async-start(f32[8,1,1,128]{3,2,1,0:T(1,128)} %constant_dynamic-update-slice_fusion.8), calls=%async_computation.1 | async-start | bytes 8192 | tf_op jit(solution)/shard_map/all_to_all | solution.py:26
